TPU v7x, 32 devices: a whole 2x2x4 slice. The times are simulated.
32 devices in a mesh: rows: 4 (over y, core), cols: 8 (over z, x).
Axes of the slice: x: 2, y: 2, z: 4, core: 2. Of those that a mesh axis runs over, the one named last changes fastest.
Arguments:
- single: bfloat16 [512, 1024], P('rows'), may hold values from -6 to 6
- pair: bfloat16 [512, 512, 128], P('rows', 'cols'), may hold values from -6 to 6
- residue_mask: int32 [512], replicated, may hold values from 0 to 1, as said below
- w_bias: bfloat16 [128, 32], replicated, may hold values from -40 to 40
- w_project: bfloat16 [4, 1024, 1024], P(None, None, 'cols'), may hold values from -0.1875 to 0.1875
- w_out: bfloat16 [1024, 1024], replicated, may hold values from -0.1875 to 0.1875
- w_factors: bfloat16 [1024, 128], replicated, may hold values from -0.1875 to 0.1875
- w_pairout: bfloat16 [128, 128], replicated, may hold values from -0.5 to 0.5
- w_up: bfloat16 [128, 512], replicated, may hold values from -0.5 to 0.5
- w_down: bfloat16 [512, 128], replicated, may hold values from -0.25 to 0.25
Outputs:
- single_out: bfloat16 [512, 1024], P('rows')
- pair_out: bfloat16 [512, 512, 128], P('rows', 'cols')
Inputs may be any that keep to these rules, and one draw needn't show every extreme that they name: residue_mask is 1 on a leading run of at least 256 positions and 0 after it.
All inputs are finite; a program needn't handle non-finite values.
Results may differ from a plain program's by a relative error of at most 0.01.
The roundings to bfloat16 on the way count: a program that leaves them out, or rounds other values in their place, can miss the bound.
Values may be sent and summed in bfloat16 or wider, within the bound.
A program may use at most 64 MiB of HBM per device.

v0:
```python
import math
import jax
import jax.numpy as jnp
from jax import lax
from jax.sharding import PartitionSpec as P

epsilon = 1e-05


def from_root(value, axis, root):
    mine = lax.axis_index(axis) == root
    return lax.psum(jnp.where(mine, value, jnp.zeros_like(value)), axis)


def layer_norm(values):
    values = values.astype(jnp.float32)
    centred = values - jnp.mean(values, -1, keepdims=True)
    return centred * lax.rsqrt(jnp.mean(centred * centred, -1, keepdims=True) + epsilon)


def per_device(
    single, pair, residue_mask, w_bias, w_project, w_out, w_factors, w_pairout, w_up, w_down
):
    tile_rows = pair.shape[0]
    tile_cols = pair.shape[1]
    normed_pair = layer_norm(pair).astype(jnp.bfloat16)
    bias_local = jnp.einsum(
        "rcp,ph->hrc", normed_pair, w_bias, preferred_element_type=jnp.float32
    ).astype(jnp.bfloat16)
    normed_single = layer_norm(single).astype(jnp.bfloat16)
    projected = jnp.einsum(
        "rs,fsc->frc", normed_single, w_project, preferred_element_type=jnp.float32
    )
    query_rows = projected[0].astype(jnp.bfloat16)
    key_local = projected[1].astype(jnp.bfloat16)
    value_local = projected[2].astype(jnp.bfloat16)
    gate_values = jax.nn.sigmoid(projected[3])
    first_residue = lax.axis_index("cols") * tile_cols
    owner_row = first_residue // tile_rows
    offset_rows = first_residue - owner_row * tile_rows
    bias_heads = lax.all_to_all(bias_local, "cols", split_axis=0, concat_axis=2, tiled=True)
    key_rows, value_rows = (
        lax.all_gather(key_local, "rows", axis=0, tiled=True),
        lax.all_gather(value_local, "rows", axis=0, tiled=True),
    )
    heads_here = bias_heads.shape[0]
    head_width = query_rows.shape[1] // heads_here
    residues = key_rows.shape[0]
    query_split = query_rows.reshape(tile_rows, heads_here, head_width)
    key_split = key_rows.reshape(residues, heads_here, head_width)
    value_split = value_rows.reshape(residues, heads_here, head_width)
    score_scale = 1.0 / math.sqrt(head_width)
    scores = jnp.einsum(
        "rhd,lhd->hrl", query_split, key_split, preferred_element_type=jnp.float32
    ) * score_scale + bias_heads.astype(jnp.float32)
    key_valid = (residue_mask > 0)[None, None, :]
    scores = jnp.where(key_valid, scores, -jnp.inf)
    weights = jax.nn.softmax(scores, axis=-1).astype(jnp.bfloat16)
    attended = jnp.einsum("hrl,lhd->rhd", weights, value_split, preferred_element_type=jnp.float32)
    attended = attended.reshape(tile_rows, heads_here * head_width)
    mixed = (attended * gate_values).astype(jnp.bfloat16)
    whole_heads = lax.all_gather(mixed, "cols", axis=1, tiled=True)
    head_total = jnp.dot(whole_heads, w_out, preferred_element_type=jnp.float32)
    single_out = (single.astype(jnp.float32) + head_total).astype(jnp.bfloat16)
    normed_out = layer_norm(single_out).astype(jnp.bfloat16)
    factors = jnp.dot(normed_out, w_factors, preferred_element_type=jnp.float32).astype(
        jnp.bfloat16
    )
    factor_width = factors.shape[1] // 2
    left_factor = factors[:, :factor_width]
    right_local = factors[:, factor_width:]
    right_piece = lax.dynamic_slice_in_dim(right_local, offset_rows, tile_cols, 0)
    right_cols = from_root(right_piece, "rows", owner_row)
    block_rows = math.gcd(tile_rows, max(1, 4096 // tile_cols))
    count_blocks = tile_rows // block_rows

    def update_block(operands):
        pair_block, left_block = operands
        left_wide = left_block.astype(jnp.float32)[:, None, :]
        right_wide = right_cols.astype(jnp.float32)[None, :, :]
        paired = jnp.concatenate([left_wide * right_wide, left_wide - right_wide], -1).astype(
            jnp.bfloat16
        )
        pair_mid = (
            pair_block.astype(jnp.float32)
            + jnp.einsum("rcq,qp->rcp", paired, w_pairout, preferred_element_type=jnp.float32)
        ).astype(jnp.bfloat16)
        normed_mid = layer_norm(pair_mid).astype(jnp.bfloat16)
        hidden = jax.nn.relu(
            jnp.einsum("rcp,pk->rck", normed_mid, w_up, preferred_element_type=jnp.float32)
        ).astype(jnp.bfloat16)
        return (
            pair_mid.astype(jnp.float32)
            + jnp.einsum("rck,kp->rcp", hidden, w_down, preferred_element_type=jnp.float32)
        ).astype(jnp.bfloat16)

    updated = lax.map(
        update_block,
        (
            pair.reshape(count_blocks, block_rows, tile_cols, pair.shape[2]),
            left_factor.reshape(count_blocks, block_rows, factor_width),
        ),
    )
    return (single_out, updated.reshape(pair.shape))


def solution(mesh):
    return jax.shard_map(
        per_device,
        mesh=mesh,
        in_specs=(
            P("rows", None),
            P("rows", "cols", None),
            P(),
            P(),
            P(None, None, "cols"),
            P(),
            P(),
            P(),
            P(),
            P(),
        ),
        out_specs=(P("rows", None), P("rows", "cols", None)),
        check_vma=False,
    )
```

profile of v0, /device:TPU:0, one launch (start us, length us, event | category | flops | bytes accessed | tf_op | source)
XLA Modules:
  0.0 100.3 jit_solution(4183967973226425376)
XLA Ops:
  0.7 2.9 %convert_reduce_fusion.1 = f32[128,64]{1,0:T(8,128)S(1)} fusion(bf16[128,64,128]{2,1,0:T(8,128)(2,1)} %param.13), kind=kLoop, calls=%fused_computation.33 | loop fusion | flops 2088960 | bytes 2129920 | tf_op jit(solution)/shard_map/reduce_sum | solution.py:17
  3.6 2.7 %fusion.30 = f32[128,64]{1,0:T(8,128)S(1)} fusion(bf16[128,64,128]{2,1,0:T(8,128)(2,1)S(1)} %copy-done.1, f32[128,64]{1,0:T(8,128)S(1)} %broadcast_multiply_fusion.1), kind=kLoop, calls=%fused_computation.36 | loop fusion | flops 4186112 | bytes 2162688 | tf_op jit(solution)/shard_map/reduce_sum | solution.py:18
  6.4 3.4 %fusion.31 = bf16[128,64,128]{2,1,0:T(8,128)(2,1)S(1)} fusion(bf16[128,64,128]{2,1,0:T(8,128)(2,1)S(1)} %copy-done.1, f32[128,64]{1,0:T(8,128)S(1)} %add_rsqrt_fusion.1, f32[128,64]{1,0:T(8,128)S(1)} %broadcast_multiply_fusion.1), kind=kLoop, calls=%fused_computation.37 | loop fusion | flops 4194304 | bytes 4259840 | tf_op jit(solution)/shard_map/convert_element_type | solution.py:26
  9.8 1.4 %fusion.41 = bf16[32,128,64]{1,0,2:T(8,128)(2,1)S(1)} fusion(bf16[128,64,128]{2,1,0:T(8,128)(2,1)S(1)} %fusion.31, bf16[128,32]{0,1:T(8,128)(2,1)S(1)} %copy-done.7), kind=kOutput, calls=%fused_computation.46 | convolution fusion | flops 67371008 | bytes 2629632 | tf_op jit(solution)/shard_map/rcp,ph->hrc/dot_general | solution.py:27
  11.1 1.0 %copy.31 = bf16[32,128,64]{1,2,0:T(8,128)(2,1)} copy(bf16[32,128,64]{1,0,2:T(8,128)(2,1)S(1)} %fusion.41) | data formatting | bytes 1048576 | tf_op jit(solution)/shard_map/convert_element_type | solution.py:29
  12.2 7.3 %all-to-all-start = ((bf16[32,128,64]{1,2,0:T(8,128)(2,1)}), bf16[32,128,64]{1,2,0:T(8,128)(2,1)}, u32[]{:S(2)}, u32[]{:S(2)}) async-start(bf16[32,128,64]{1,2,0:T(8,128)(2,1)} %copy.31), calls=%async_computation | async-start | bytes 1048576 | tf_op jit(solution)/shard_map/all_to_all | solution.py:41
  19.9 1.5 %copy.29 = bf16[4,1024,128]{1,2,0:T(8,128)(2,1)S(1)} copy(bf16[4,1024,128]{2,1,0:T(8,128)(2,1)} %param.16) | data formatting | bytes 2097152 | tf_op args[4]
  21.3 0.5 fusion.55
  21.9 0.7 copy-done.4
  22.6 0.6 fusion.69
  23.2 5.4 %all-gather.1 = bf16[1,512,128]{1,2,0:T(8,128)(2,1)S(1)} all-gather(bf16[1,128,128]{1,2,0:T(8,128)(2,1)S(1)} %get-tuple-element.97), channel_id=3, replica_groups=mesh['rows'=4,'cols'=8] {'rows'}, dimensions={1}, use_global_device_ids=true | all-gather | bytes 163840 | tf_op jit(solution)/shard_map/all_gather | solution.py:43
  28.7 5.9 %all-gather = bf16[1,512,128]{1,2,0:T(8,128)(2,1)} all-gather(bf16[1,128,128]{1,2,0:T(8,128)(2,1)S(1)} %get-tuple-element.99), channel_id=2, replica_groups=mesh['rows'=4,'cols'=8] {'rows'}, dimensions={1}, use_global_device_ids=true | all-gather | bytes 163840 | tf_op jit(solution)/shard_map/all_gather | solution.py:44
  34.5 1.1 %convert_bitcast_fusion = f32[4,128,8,64]{1,3,0,2:T(8,128)S(1)} fusion(bf16[8,4,128,64]{2,3,1,0:T(8,128)(2,1)} %bitcast.28), kind=kLoop, calls=%fused_computation.50 | loop fusion | flops 262144 | bytes 1572864 | tf_op jit(solution)/shard_map/convert_element_type | solution.py:55
  35.8 1.3 %copy.33 = f32[4,128,512]{2,1,0:T(8,128)} copy(f32[4,128,512]{1,2,0:T(8,128)S(1)} %bitcast.77) | data formatting | bytes 2097152 | tf_op jit(solution)/shard_map/convert_element_type | solution.py:55
  37.1 1.6 %fusion.37 = f32[4,128,512]{2,1,0:T(8,128)S(1)} fusion(f32[4,128,512]{2,1,0:T(8,128)} %copy.33, bf16[128,4,32]{0,2,1:T(8,128)(2,1)} %bitcast.82, bf16[512,4,32]{0,2,1:T(8,128)(2,1)S(1)} %bitcast.80, pred[512]{0:T(512)(128)(4,1)S(1)} %broadcast_compare_fusion), kind=kOutput, calls=%fused_computation.44 | convolution fusion | flops 17563648 | bytes 2261504 | tf_op jit(solution)/shard_map/rhd,lhd->hrl/dot_general | solution.py:53
  39.0 1.9 %fusion.53 = f32[4,32,128]{2,1,0:T(8,128)S(1)} fusion(bf16[512,4,32]{0,2,1:T(8,128)(2,1)} %bitcast.83, f32[4,128]{1,0:T(4,128)S(1)} %fusion.71, f32[4,128,512]{2,1,0:T(8,128)S(1)} %fusion.37), kind=kOutput, calls=%fused_computation.64 | convolution fusion | flops 17564672 | bytes 1247232 | tf_op jit(solution)/shard_map/hrl,lhd->rhd/dot_general | solution.py:59
  41.0 0.9 fusion.66
  41.9 31.5 %all_gather.11 = bf16[128,1024]{0,1:T(8,128)(2,1)S(1)} all-gather(bf16[128,128]{0,1:T(8,128)(2,1)S(1)} %fusion.66), channel_id=1, replica_groups=mesh['rows'=4,'cols'=8] {'cols'}, dimensions={1}, use_global_device_ids=true | all-gather | bytes 294912 | tf_op jit(solution)/shard_map/all_gather | solution.py:62
  73.4 0.5 convert_reduce_fusion.3
  74.2 0.3 convolution_convert_fusion
  74.7 10.3 %psum.7 = bf16[64,64]{0,1:T(8,128)(2,1)S(1)} all-reduce(bf16[64,64]{0,1:T(8,128)(2,1)S(1)} %dynamic-slice_select_fusion), channel_id=1, replica_groups=mesh['rows'=4,'cols'=8] {'rows'}, use_global_device_ids=true, to_apply=%region_8.9 | all-reduce | flops 4096 | bytes 16384 | tf_op jit(solution)/shard_map/psum | solution.py:12
  85.2 15.0 %while.10 = (s32[]{:T(128)}, bf16[2,64,64,128]{3,2,1,0:T(8,128)(2,1)}, bf16[2,64,64,128]{3,2,1,0:T(8,128)(2,1)}, bf16[2,64,64]{2,1,0:T(8,128)(2,1)S(1)}, bf16[64...) while((s32[]{:T(128)}, ...), condition=%wide.region_12.13_spmd, body=%wide.region_9.12_spmd.sunk | while | flops 1223700480 | bytes 17334912 | solution.py:97
  85.3 0.5 multiply_convert_fusion.2
  85.8 1.0 copy-done.2
  86.8 1.2 %convert_reduce_fusion.5 = (f32[64,64]{1,0:T(8,128)S(1)}, bf16[64,64,128]{2,1,0:T(8,128)(2,1)S(1)}) fusion(bf16[128,128]{1,0:T(8,128)(2,1)S(1)} %get-tuple-element.184, bf16[64,64,64]{2,1,0:T(8,128)(2,1)S(1)} %get-tuple-element.157, bf16[64,64,64]{2,1,0:T(8,128)(2,1)S(1)} %get-tuple-element.158, bf16[2,64,64,128]{3,2,1,0:T(8,128)(2,1)S(1)} %copy-done.2, ...), kind=kOutput, calls=%fused_computation.6.clone.1 | convolution fusion | flops 138932224 | bytes 3194884 | tf_op jit(solution)/shard_map/while/body/eval_jaxpr/rcq,qp->rcp/dot_general | solution.py:86
  88.1 1.3 %fusion.89 = f32[64,64]{1,0:T(8,128)S(1)} fusion(bf16[64,64,128]{2,1,0:T(8,128)(2,1)S(1)} %get-tuple-element.159, f32[64,64]{1,0:T(8,128)S(1)} %broadcast_multiply_fusion.5), kind=kLoop, calls=%fused_computation.9.clone.1 | loop fusion | flops 2093056 | bytes 1081344 | tf_op jit(solution)/shard_map/while/body/eval_jaxpr/reduce_sum | solution.py:18
  89.4 3.4 %fusion.90 = bf16[2,64,64,128]{3,2,1,0:T(8,128)(2,1)} fusion(bf16[2,64,64,128]{3,2,1,0:T(8,128)(2,1)} %get-tuple-element.171, s32[]{:T(128)} %get-tuple-element.170, bf16[64,64,128]{2,1,0:T(8,128)(2,1)S(1)} %get-tuple-element.159, f32[64,64]{1,0:T(8,128)S(1)} %add_rsqrt_fusion.5, f32[64,64]{1,0:T(8,128)S(1)} %broadcast_multiply_fusion.5, ...), kind=kOutput, calls=%fused_computation.17.clone.1 | convolution fusion | flops 1081606144 | bytes 3473920 | tf_op jit(solution)/shard_map/while/body/eval_jaxpr/rck,kp->rcp/dot_general | solution.py:94
  92.8 0.5 multiply_convert_fusion.2
  93.3 1.0 %copy-done.2 = bf16[2,64,64,128]{3,2,1,0:T(8,128)(2,1)S(1)} copy-done((bf16[2,64,64,128]{3,2,1,0:T(8,128)(2,1)S(1)}, bf16[2,64,64,128]{3,2,1,0:T(8,128)(2,1)}, u32[]{:S(2)}) %copy-start.2) | copy-done | bytes 2097176 | tf_op jit(solution)/shard_map/while
  94.4 1.2 %convert_reduce_fusion.5 = (f32[64,64]{1,0:T(8,128)S(1)}, bf16[64,64,128]{2,1,0:T(8,128)(2,1)S(1)}) fusion(bf16[128,128]{1,0:T(8,128)(2,1)S(1)} %get-tuple-element.184, bf16[64,64,64]{2,1,0:T(8,128)(2,1)S(1)} %get-tuple-element.157, bf16[64,64,64]{2,1,0:T(8,128)(2,1)S(1)} %get-tuple-element.158, bf16[2,64,64,128]{3,2,1,0:T(8,128)(2,1)S(1)} %copy-done.2, ...), kind=kOutput, calls=%fused_computation.6.clone.1 | convolution fusion | flops 138932224 | bytes 3194884 | tf_op jit(solution)/shard_map/while/body/eval_jaxpr/rcq,qp->rcp/dot_general | solution.py:86
  95.6 1.3 %fusion.89 = f32[64,64]{1,0:T(8,128)S(1)} fusion(bf16[64,64,128]{2,1,0:T(8,128)(2,1)S(1)} %get-tuple-element.159, f32[64,64]{1,0:T(8,128)S(1)} %broadcast_multiply_fusion.5), kind=kLoop, calls=%fused_computation.9.clone.1 | loop fusion | flops 2093056 | bytes 1081344 | tf_op jit(solution)/shard_map/while/body/eval_jaxpr/reduce_sum | solution.py:18
  96.9 3.4 %fusion.90 = bf16[2,64,64,128]{3,2,1,0:T(8,128)(2,1)} fusion(bf16[2,64,64,128]{3,2,1,0:T(8,128)(2,1)} %get-tuple-element.171, s32[]{:T(128)} %get-tuple-element.170, bf16[64,64,128]{2,1,0:T(8,128)(2,1)S(1)} %get-tuple-element.159, f32[64,64]{1,0:T(8,128)S(1)} %add_rsqrt_fusion.5, f32[64,64]{1,0:T(8,128)S(1)} %broadcast_multiply_fusion.5, ...), kind=kOutput, calls=%fused_computation.17.clone.1 | convolution fusion | flops 1081606144 | bytes 3473920 | tf_op jit(solution)/shard_map/while/body/eval_jaxpr/rck,kp->rcp/dot_general | solution.py:94
  (50 shorter events, 1.4 us)
Async XLA Ops:
  0.6 72.8 %copy-start = (bf16[1024,1024]{1,0:T(8,128)(2,1)S(1)}, bf16[1024,1024]{1,0:T(8,128)(2,1)}, u32[]{:S(2)}) copy-start(bf16[1024,1024]{1,0:T(8,128)(2,1)} %param.17) | copy-start | bytes 6291460
  0.6 2.9 %copy-start.1 = (bf16[128,64,128]{2,1,0:T(8,128)(2,1)S(1)}, bf16[128,64,128]{2,1,0:T(8,128)(2,1)}, u32[]{:S(2)}) copy-start(bf16[128,64,128]{2,1,0:T(8,128)(2,1)} %param.13) | copy-start | bytes 6291460
  6.4 3.4 %copy-start.7 = (bf16[128,32]{0,1:T(8,128)(2,1)S(1)}, bf16[128,32]{0,1:T(8,128)(2,1)}, u32[]{:S(2)}) copy-start(bf16[128,32]{0,1:T(8,128)(2,1)} %param.15) | copy-start | bytes 24580
  9.7 9.7 %copy-start.3 = (bf16[128,1024]{1,0:T(8,128)(2,1)S(1)}, bf16[128,1024]{1,0:T(8,128)(2,1)}, u32[]{:S(2)}) copy-start(bf16[128,1024]{1,0:T(8,128)(2,1)} %param.12) | copy-start | bytes 786436
  12.2 22.4 %all-to-all-start = ((bf16[32,128,64]{1,2,0:T(8,128)(2,1)}), bf16[32,128,64]{1,2,0:T(8,128)(2,1)}, u32[]{:S(2)}, u32[]{:S(2)}) async-start(bf16[32,128,64]{1,2,0:T(8,128)(2,1)} %copy.31), calls=%async_computation | async-start | bytes 1048576 | tf_op jit(solution)/shard_map/all_to_all | solution.py:41
  19.8 14.7 %copy-start.8 = (s32[512]{0:T(512)S(1)}, s32[512]{0:T(512)}, u32[]{:S(2)}) copy-start(s32[512]{0:T(512)} %param.14) | copy-start | bytes 6148
  21.9 0.7 copy-start.4
  41.0 33.3 %copy-start.9 = (bf16[1024,128]{1,0:T(8,128)(2,1)S(1)}, bf16[1024,128]{1,0:T(8,128)(2,1)}, u32[]{:S(2)}) copy-start(bf16[1024,128]{1,0:T(8,128)(2,1)} %param.18) | copy-start | bytes 786436
  41.9 43.3 %copy-start.6 = (bf16[128,128]{1,0:T(8,128)(2,1)S(1)}, bf16[128,128]{1,0:T(8,128)(2,1)}, u32[]{:S(2)}) copy-start(bf16[128,128]{1,0:T(8,128)(2,1)} %param.19) | copy-start | bytes 98308
  41.9 43.3 %copy-start.10 = (bf16[128,512]{1,0:T(8,128)(2,1)S(1)}, bf16[128,512]{1,0:T(8,128)(2,1)}, u32[]{:S(2)}) copy-start(bf16[128,512]{1,0:T(8,128)(2,1)} %param.20) | copy-start | bytes 393220
  41.9 43.3 %copy-start.11 = (bf16[512,128]{1,0:T(8,128)(2,1)S(1)}, bf16[512,128]{1,0:T(8,128)(2,1)}, u32[]{:S(2)}) copy-start(bf16[512,128]{1,0:T(8,128)(2,1)} %param.21) | copy-start | bytes 393220
  74.0 11.2 %copy-start.5 = (bf16[128,1024]{1,0:T(8,128)(2,1)}, bf16[128,1024]{1,0:T(8,128)(2,1)S(1)}, u32[]{:S(2)}) copy-start(bf16[128,1024]{1,0:T(8,128)(2,1)S(1)} %get-tuple-element.103) | copy-start | bytes 786436
  85.2 1.6 %copy-start.2 = (bf16[2,64,64,128]{3,2,1,0:T(8,128)(2,1)S(1)}, bf16[2,64,64,128]{3,2,1,0:T(8,128)(2,1)}, u32[]{:S(2)}) copy-start(bf16[2,64,64,128]{3,2,1,0:T(8,128)(2,1)} %get-tuple-element.181) | copy-start | bytes 6291460 | tf_op jit(solution)/shard_map/while
  92.8 1.6 %copy-start.2 = (bf16[2,64,64,128]{3,2,1,0:T(8,128)(2,1)S(1)}, bf16[2,64,64,128]{3,2,1,0:T(8,128)(2,1)}, u32[]{:S(2)}) copy-start(bf16[2,64,64,128]{3,2,1,0:T(8,128)(2,1)} %get-tuple-element.181) | copy-start | bytes 6291460 | tf_op jit(solution)/shard_map/while
where the time goes:
time: 101 us; the launch traced here: 100 us
  blocking collectives  53.1 us (53%)
  other arithmetic  15.9 us (16%)
  matrix products  15.5 us (15%)
  local copies, waits for them, and re-layouts  7.51 us (7%)
  starting transfers between devices  7.28 us (7%)
    all_gather x1, blocking collectives, per_device(): whole_heads = lax.all_gather(mixed, 'cols', axis=1, tiled=True)  31.5 us
    psum x1, blocking collectives, from_root(): return lax.psum(jnp.where(mine, value, jnp.zeros_like(value)), axis)  10.3 us
    all_to_all x1, starting transfers between devices, per_device(): lax.all_to_all(bias_local, 'cols', split_axis=0, concat_axis=2, tiled=True)  7.28 us
    dot_general x2, matrix products, update_block(): jnp.einsum('rck,kp->rcp', hidden, w_down, preferred_element_type=jnp.floa...  6.75 us
    all_gather x1, blocking collectives, per_device(): lax.all_gather(value_local, 'rows', axis=0, tiled=True)  5.88 us
    reduce_sum x5, other arithmetic, layer_norm(): jnp.mean(centred * centred, -1, keepdims=True) + epsilon  5.77 us
    all_gather x1, blocking collectives, per_device(): lax.all_gather(key_local, 'rows', axis=0, tiled=True)  5.43 us
    convert_element_type x1, other arithmetic, per_device(): normed_pair = layer_norm(pair).astype(jnp.bfloat16)  3.36 us
  transfers between devices with their start and end apart: 1, of which 0 were waited for; matrix products, arithmetic and copies ran while one was open for 3% of the time, Pallas kernels for 0%

commit v1 on v0

--- a/solution.py
+++ b/solution.py
@@ -9,7 +9,7 @@
 
 def from_root(value, axis, root):
     mine = lax.axis_index(axis) == root
-    return lax.psum(jnp.where(mine, value, jnp.zeros_like(value)), axis)
+    return jnp.sum(lax.all_gather(jnp.where(mine, value, jnp.zeros_like(value)), axis), axis=0)
 
 
 def layer_norm(values):

time: 101 us -> 95.7 us (0.948)
  blocking collectives: 53.1 us -> 48.1 us
    psum x1 -> x0, blocking collectives: 10.3 us -> none  [from_root(): return lax.psum(jnp.where(mine, value, jnp.zeros_like(value)), axis)]
    all_gather x0 -> x1, blocking collectives: none -> 5.42 us  [from_root(): lax.all_gather(jnp.where(mine, value, jnp.zeros_like(value)), axis)]
where the time goes in v1:
time: 95.7 us; the launch traced here: 95.3 us
  blocking collectives  48.1 us (50%)
  other arithmetic  15.9 us (17%)
  matrix products  15.5 us (16%)
  local copies, waits for them, and re-layouts  7.5 us (8%)
  starting transfers between devices  7.28 us (8%)
    all_gather x1, blocking collectives, per_device(): whole_heads = lax.all_gather(mixed, 'cols', axis=1, tiled=True)  31.4 us
    all_to_all x1, starting transfers between devices, per_device(): lax.all_to_all(bias_local, 'cols', split_axis=0, concat_axis=2, tiled=True)  7.28 us
    dot_general x2, matrix products, update_block(): jnp.einsum('rck,kp->rcp', hidden, w_down, preferred_element_type=jnp.floa...  6.76 us
    all_gather x1, blocking collectives, per_device(): lax.all_gather(value_local, 'rows', axis=0, tiled=True)  5.88 us
    reduce_sum x5, other arithmetic, layer_norm(): jnp.mean(centred * centred, -1, keepdims=True) + epsilon  5.77 us
    all_gather x1, blocking collectives, per_device(): lax.all_gather(key_local, 'rows', axis=0, tiled=True)  5.43 us
    all_gather x1, blocking collectives, from_root(): lax.all_gather(jnp.where(mine, value, jnp.zeros_like(value)), axis)  5.42 us
    convert_element_type x1, other arithmetic, per_device(): normed_pair = layer_norm(pair).astype(jnp.bfloat16)  3.36 us
  transfers between devices with their start and end apart: 1, of which 0 were waited for; matrix products, arithmetic and copies ran while one was open for 3% of the time, Pallas kernels for 0%

profile of v1, /device:TPU:0, one launch (start us, length us, event | category | flops | bytes accessed | tf_op | source)
XLA Modules:
  0.0 95.3 jit_solution(412793346455693006)
XLA Ops:
  0.7 2.9 %convert_reduce_fusion.1 = f32[128,64]{1,0:T(8,128)S(1)} fusion(bf16[128,64,128]{2,1,0:T(8,128)(2,1)} %param.13), kind=kLoop, calls=%fused_computation.33 | loop fusion | flops 2088960 | bytes 2129920 | tf_op jit(solution)/shard_map/reduce_sum | solution.py:17
  3.6 2.7 %fusion.30 = f32[128,64]{1,0:T(8,128)S(1)} fusion(bf16[128,64,128]{2,1,0:T(8,128)(2,1)S(1)} %copy-done.1, f32[128,64]{1,0:T(8,128)S(1)} %broadcast_multiply_fusion.1), kind=kLoop, calls=%fused_computation.36 | loop fusion | flops 4186112 | bytes 2162688 | tf_op jit(solution)/shard_map/reduce_sum | solution.py:18
  6.4 3.4 %fusion.31 = bf16[128,64,128]{2,1,0:T(8,128)(2,1)S(1)} fusion(bf16[128,64,128]{2,1,0:T(8,128)(2,1)S(1)} %copy-done.1, f32[128,64]{1,0:T(8,128)S(1)} %add_rsqrt_fusion.1, f32[128,64]{1,0:T(8,128)S(1)} %broadcast_multiply_fusion.1), kind=kLoop, calls=%fused_computation.37 | loop fusion | flops 4194304 | bytes 4259840 | tf_op jit(solution)/shard_map/convert_element_type | solution.py:26
  9.8 1.4 %fusion.41 = bf16[32,128,64]{1,0,2:T(8,128)(2,1)S(1)} fusion(bf16[128,64,128]{2,1,0:T(8,128)(2,1)S(1)} %fusion.31, bf16[128,32]{0,1:T(8,128)(2,1)S(1)} %copy-done.7), kind=kOutput, calls=%fused_computation.46 | convolution fusion | flops 67371008 | bytes 2629632 | tf_op jit(solution)/shard_map/rcp,ph->hrc/dot_general | solution.py:27
  11.1 1.0 %copy.31 = bf16[32,128,64]{1,2,0:T(8,128)(2,1)} copy(bf16[32,128,64]{1,0,2:T(8,128)(2,1)S(1)} %fusion.41) | data formatting | bytes 1048576 | tf_op jit(solution)/shard_map/convert_element_type | solution.py:29
  12.2 7.3 %all-to-all-start = ((bf16[32,128,64]{1,2,0:T(8,128)(2,1)}), bf16[32,128,64]{1,2,0:T(8,128)(2,1)}, u32[]{:S(2)}, u32[]{:S(2)}) async-start(bf16[32,128,64]{1,2,0:T(8,128)(2,1)} %copy.31), calls=%async_computation | async-start | bytes 1048576 | tf_op jit(solution)/shard_map/all_to_all | solution.py:41
  19.9 1.5 %copy.29 = bf16[4,1024,128]{1,2,0:T(8,128)(2,1)S(1)} copy(bf16[4,1024,128]{2,1,0:T(8,128)(2,1)} %param.16) | data formatting | bytes 2097152 | tf_op args[4]
  21.3 0.5 fusion.55
  21.9 0.7 copy-done.4
  22.6 0.6 fusion.69
  23.2 5.4 %all-gather.1 = bf16[1,512,128]{1,2,0:T(8,128)(2,1)S(1)} all-gather(bf16[1,128,128]{1,2,0:T(8,128)(2,1)S(1)} %get-tuple-element.97), channel_id=3, replica_groups=mesh['rows'=4,'cols'=8] {'rows'}, dimensions={1}, use_global_device_ids=true | all-gather | bytes 163840 | tf_op jit(solution)/shard_map/all_gather | solution.py:43
  28.7 5.9 %all-gather = bf16[1,512,128]{1,2,0:T(8,128)(2,1)} all-gather(bf16[1,128,128]{1,2,0:T(8,128)(2,1)S(1)} %get-tuple-element.99), channel_id=2, replica_groups=mesh['rows'=4,'cols'=8] {'rows'}, dimensions={1}, use_global_device_ids=true | all-gather | bytes 163840 | tf_op jit(solution)/shard_map/all_gather | solution.py:44
  34.5 1.1 %convert_bitcast_fusion = f32[4,128,8,64]{1,3,0,2:T(8,128)S(1)} fusion(bf16[8,4,128,64]{2,3,1,0:T(8,128)(2,1)} %bitcast.29), kind=kLoop, calls=%fused_computation.50 | loop fusion | flops 262144 | bytes 1572864 | tf_op jit(solution)/shard_map/convert_element_type | solution.py:55
  35.8 1.3 %copy.33 = f32[4,128,512]{2,1,0:T(8,128)} copy(f32[4,128,512]{1,2,0:T(8,128)S(1)} %bitcast.78) | data formatting | bytes 2097152 | tf_op jit(solution)/shard_map/convert_element_type | solution.py:55
  37.1 1.6 %fusion.37 = f32[4,128,512]{2,1,0:T(8,128)S(1)} fusion(f32[4,128,512]{2,1,0:T(8,128)} %copy.33, bf16[128,4,32]{0,2,1:T(8,128)(2,1)} %bitcast.84, bf16[512,4,32]{0,2,1:T(8,128)(2,1)S(1)} %bitcast.81, pred[512]{0:T(512)(128)(4,1)S(1)} %broadcast_compare_fusion), kind=kOutput, calls=%fused_computation.44 | convolution fusion | flops 17563648 | bytes 2261504 | tf_op jit(solution)/shard_map/rhd,lhd->hrl/dot_general | solution.py:53
  39.0 1.9 %fusion.53 = f32[4,32,128]{2,1,0:T(8,128)S(1)} fusion(bf16[512,4,32]{0,2,1:T(8,128)(2,1)} %bitcast.85, f32[4,128]{1,0:T(4,128)S(1)} %fusion.71, f32[4,128,512]{2,1,0:T(8,128)S(1)} %fusion.37), kind=kOutput, calls=%fused_computation.64 | convolution fusion | flops 17564672 | bytes 1247232 | tf_op jit(solution)/shard_map/hrl,lhd->rhd/dot_general | solution.py:59
  41.0 0.9 fusion.66
  41.9 31.4 %all_gather.17 = bf16[128,1024]{0,1:T(8,128)(2,1)S(1)} all-gather(bf16[128,128]{0,1:T(8,128)(2,1)S(1)} %fusion.66), channel_id=1, replica_groups=mesh['rows'=4,'cols'=8] {'cols'}, dimensions={1}, use_global_device_ids=true | all-gather | bytes 294912 | tf_op jit(solution)/shard_map/all_gather | solution.py:62
  73.3 0.5 convert_reduce_fusion.3
  74.1 0.3 convolution_convert_fusion
  74.6 5.4 %all-gather.2 = bf16[256,64]{1,0:T(8,128)(2,1)S(1)} all-gather(bf16[64,64]{1,0:T(8,128)(2,1)S(1)} %copy.34), channel_id=4, replica_groups=mesh['rows'=4,'cols'=8] {'rows'}, dimensions={0}, use_global_device_ids=true | all-gather | bytes 40960 | tf_op jit(solution)/shard_map/all_gather | solution.py:12
  80.2 15.1 %while.10 = (s32[]{:T(128)}, bf16[2,64,64,128]{3,2,1,0:T(8,128)(2,1)}, bf16[2,64,64,128]{3,2,1,0:T(8,128)(2,1)}, bf16[2,64,64]{2,1,0:T(8,128)(2,1)S(1)}, bf16[64...) while((s32[]{:T(128)}, ...), condition=%wide.region_12.13_spmd, body=%wide.region_9.12_spmd.sunk | while | flops 1223700480 | bytes 17334912 | solution.py:97
  80.3 0.5 multiply_convert_fusion.2
  80.8 1.0 %copy-done.2 = bf16[2,64,64,128]{3,2,1,0:T(8,128)(2,1)S(1)} copy-done((bf16[2,64,64,128]{3,2,1,0:T(8,128)(2,1)S(1)}, bf16[2,64,64,128]{3,2,1,0:T(8,128)(2,1)}, u32[]{:S(2)}) %copy-start.2) | copy-done | bytes 2097176 | tf_op jit(solution)/shard_map/while
  81.8 1.2 %convert_reduce_fusion.5 = (f32[64,64]{1,0:T(8,128)S(1)}, bf16[64,64,128]{2,1,0:T(8,128)(2,1)S(1)}) fusion(bf16[128,128]{1,0:T(8,128)(2,1)S(1)} %get-tuple-element.184, bf16[64,64,64]{2,1,0:T(8,128)(2,1)S(1)} %get-tuple-element.157, bf16[64,64,64]{2,1,0:T(8,128)(2,1)S(1)} %get-tuple-element.158, bf16[2,64,64,128]{3,2,1,0:T(8,128)(2,1)S(1)} %copy-done.2, ...), kind=kOutput, calls=%fused_computation.6.clone.1 | convolution fusion | flops 138932224 | bytes 3194884 | tf_op jit(solution)/shard_map/while/body/eval_jaxpr/rcq,qp->rcp/dot_general | solution.py:86
  83.1 1.3 %fusion.89 = f32[64,64]{1,0:T(8,128)S(1)} fusion(bf16[64,64,128]{2,1,0:T(8,128)(2,1)S(1)} %get-tuple-element.159, f32[64,64]{1,0:T(8,128)S(1)} %broadcast_multiply_fusion.5), kind=kLoop, calls=%fused_computation.9.clone.1 | loop fusion | flops 2093056 | bytes 1081344 | tf_op jit(solution)/shard_map/while/body/eval_jaxpr/reduce_sum | solution.py:18
  84.4 3.4 %fusion.90 = bf16[2,64,64,128]{3,2,1,0:T(8,128)(2,1)} fusion(bf16[2,64,64,128]{3,2,1,0:T(8,128)(2,1)} %get-tuple-element.171, s32[]{:T(128)} %get-tuple-element.170, bf16[64,64,128]{2,1,0:T(8,128)(2,1)S(1)} %get-tuple-element.159, f32[64,64]{1,0:T(8,128)S(1)} %add_rsqrt_fusion.5, f32[64,64]{1,0:T(8,128)S(1)} %broadcast_multiply_fusion.5, ...), kind=kOutput, calls=%fused_computation.17.clone.1 | convolution fusion | flops 1081606144 | bytes 3473920 | tf_op jit(solution)/shard_map/while/body/eval_jaxpr/rck,kp->rcp/dot_general | solution.py:94
  87.8 0.5 multiply_convert_fusion.2
  88.3 1.0 %copy-done.2 = bf16[2,64,64,128]{3,2,1,0:T(8,128)(2,1)S(1)} copy-done((bf16[2,64,64,128]{3,2,1,0:T(8,128)(2,1)S(1)}, bf16[2,64,64,128]{3,2,1,0:T(8,128)(2,1)}, u32[]{:S(2)}) %copy-start.2) | copy-done | bytes 2097176 | tf_op jit(solution)/shard_map/while
  89.4 1.2 %convert_reduce_fusion.5 = (f32[64,64]{1,0:T(8,128)S(1)}, bf16[64,64,128]{2,1,0:T(8,128)(2,1)S(1)}) fusion(bf16[128,128]{1,0:T(8,128)(2,1)S(1)} %get-tuple-element.184, bf16[64,64,64]{2,1,0:T(8,128)(2,1)S(1)} %get-tuple-element.157, bf16[64,64,64]{2,1,0:T(8,128)(2,1)S(1)} %get-tuple-element.158, bf16[2,64,64,128]{3,2,1,0:T(8,128)(2,1)S(1)} %copy-done.2, ...), kind=kOutput, calls=%fused_computation.6.clone.1 | convolution fusion | flops 138932224 | bytes 3194884 | tf_op jit(solution)/shard_map/while/body/eval_jaxpr/rcq,qp->rcp/dot_general | solution.py:86
  90.6 1.3 %fusion.89 = f32[64,64]{1,0:T(8,128)S(1)} fusion(bf16[64,64,128]{2,1,0:T(8,128)(2,1)S(1)} %get-tuple-element.159, f32[64,64]{1,0:T(8,128)S(1)} %broadcast_multiply_fusion.5), kind=kLoop, calls=%fused_computation.9.clone.1 | loop fusion | flops 2093056 | bytes 1081344 | tf_op jit(solution)/shard_map/while/body/eval_jaxpr/reduce_sum | solution.py:18
  91.9 3.4 %fusion.90 = bf16[2,64,64,128]{3,2,1,0:T(8,128)(2,1)} fusion(bf16[2,64,64,128]{3,2,1,0:T(8,128)(2,1)} %get-tuple-element.171, s32[]{:T(128)} %get-tuple-element.170, bf16[64,64,128]{2,1,0:T(8,128)(2,1)S(1)} %get-tuple-element.159, f32[64,64]{1,0:T(8,128)S(1)} %add_rsqrt_fusion.5, f32[64,64]{1,0:T(8,128)S(1)} %broadcast_multiply_fusion.5, ...), kind=kOutput, calls=%fused_computation.17.clone.1 | convolution fusion | flops 1081606144 | bytes 3473920 | tf_op jit(solution)/shard_map/while/body/eval_jaxpr/rck,kp->rcp/dot_general | solution.py:94
  (51 shorter events, 1.5 us)
Async XLA Ops:
  0.6 72.6 %copy-start = (bf16[1024,1024]{1,0:T(8,128)(2,1)S(1)}, bf16[1024,1024]{1,0:T(8,128)(2,1)}, u32[]{:S(2)}) copy-start(bf16[1024,1024]{1,0:T(8,128)(2,1)} %param.17) | copy-start | bytes 6291460
  0.6 2.9 %copy-start.1 = (bf16[128,64,128]{2,1,0:T(8,128)(2,1)S(1)}, bf16[128,64,128]{2,1,0:T(8,128)(2,1)}, u32[]{:S(2)}) copy-start(bf16[128,64,128]{2,1,0:T(8,128)(2,1)} %param.13) | copy-start | bytes 6291460
  6.4 3.4 %copy-start.7 = (bf16[128,32]{0,1:T(8,128)(2,1)S(1)}, bf16[128,32]{0,1:T(8,128)(2,1)}, u32[]{:S(2)}) copy-start(bf16[128,32]{0,1:T(8,128)(2,1)} %param.15) | copy-start | bytes 24580
  9.7 9.7 %copy-start.3 = (bf16[128,1024]{1,0:T(8,128)(2,1)S(1)}, bf16[128,1024]{1,0:T(8,128)(2,1)}, u32[]{:S(2)}) copy-start(bf16[128,1024]{1,0:T(8,128)(2,1)} %param.12) | copy-start | bytes 786436
  12.2 22.4 %all-to-all-start = ((bf16[32,128,64]{1,2,0:T(8,128)(2,1)}), bf16[32,128,64]{1,2,0:T(8,128)(2,1)}, u32[]{:S(2)}, u32[]{:S(2)}) async-start(bf16[32,128,64]{1,2,0:T(8,128)(2,1)} %copy.31), calls=%async_computation | async-start | bytes 1048576 | tf_op jit(solution)/shard_map/all_to_all | solution.py:41
  19.8 14.7 %copy-start.8 = (s32[512]{0:T(512)S(1)}, s32[512]{0:T(512)}, u32[]{:S(2)}) copy-start(s32[512]{0:T(512)} %param.14) | copy-start | bytes 6148
  21.9 0.7 copy-start.4
  41.0 33.1 %copy-start.9 = (bf16[1024,128]{1,0:T(8,128)(2,1)S(1)}, bf16[1024,128]{1,0:T(8,128)(2,1)}, u32[]{:S(2)}) copy-start(bf16[1024,128]{1,0:T(8,128)(2,1)} %param.18) | copy-start | bytes 786436
  73.3 6.9 %copy-start.6 = (bf16[128,128]{1,0:T(8,128)(2,1)S(1)}, bf16[128,128]{1,0:T(8,128)(2,1)}, u32[]{:S(2)}) copy-start(bf16[128,128]{1,0:T(8,128)(2,1)} %param.19) | copy-start | bytes 98308
  73.3 6.9 %copy-start.10 = (bf16[128,512]{1,0:T(8,128)(2,1)S(1)}, bf16[128,512]{1,0:T(8,128)(2,1)}, u32[]{:S(2)}) copy-start(bf16[128,512]{1,0:T(8,128)(2,1)} %param.20) | copy-start | bytes 393220
  73.3 6.9 %copy-start.11 = (bf16[512,128]{1,0:T(8,128)(2,1)S(1)}, bf16[512,128]{1,0:T(8,128)(2,1)}, u32[]{:S(2)}) copy-start(bf16[512,128]{1,0:T(8,128)(2,1)} %param.21) | copy-start | bytes 393220
  73.8 6.4 %copy-start.5 = (bf16[128,1024]{1,0:T(8,128)(2,1)}, bf16[128,1024]{1,0:T(8,128)(2,1)S(1)}, u32[]{:S(2)}) copy-start(bf16[128,1024]{1,0:T(8,128)(2,1)S(1)} %get-tuple-element.103) | copy-start | bytes 786436
  80.2 1.6 %copy-start.2 = (bf16[2,64,64,128]{3,2,1,0:T(8,128)(2,1)S(1)}, bf16[2,64,64,128]{3,2,1,0:T(8,128)(2,1)}, u32[]{:S(2)}) copy-start(bf16[2,64,64,128]{3,2,1,0:T(8,128)(2,1)} %get-tuple-element.181) | copy-start | bytes 6291460 | tf_op jit(solution)/shard_map/while
  87.8 1.6 %copy-start.2 = (bf16[2,64,64,128]{3,2,1,0:T(8,128)(2,1)S(1)}, bf16[2,64,64,128]{3,2,1,0:T(8,128)(2,1)}, u32[]{:S(2)}) copy-start(bf16[2,64,64,128]{3,2,1,0:T(8,128)(2,1)} %get-tuple-element.181) | copy-start | bytes 6291460 | tf_op jit(solution)/shard_map/while
